TPU v7x, 32 devices: a whole 2x2x4 slice. The times are simulated.
32 devices in a mesh: blk: 2 (over x), tp: 4 (over z), qg: 4 (over y, core).
Axes of the slice: x: 2, y: 2, z: 4, core: 2. Of those that a mesh axis runs over, the one named last changes fastest.
Arguments:
- hidden_states: bfloat16 [1536, 4096], P(('blk', 'tp'), 'qg'), may hold values from -8 to 8
- query_states: bfloat16 [256, 4096], P('tp', 'qg'), may hold values from -8 to 8
- w_query: bfloat16 [4096, 4096], P('qg', 'tp'), may hold values from -0.25 to 0.25
- w_key: bfloat16 [4096, 1024], P('qg', 'tp'), may hold values from -0.09375 to 0.09375
- w_value: bfloat16 [4096, 1024], P('qg', 'tp'), may hold values from -0.09375 to 0.09375
- slot_order: int32 [4], replicated, may hold values from 0 to 3, each once
Outputs:
- attention: bfloat16 [1536, 4096], P(('blk', 'qg'), 'tp')
- decoded: bfloat16 [256, 4096], P('qg', 'tp')
Inputs may be any that keep to these rules, and one draw needn't show every extreme that they name: slot_order holds every number of 0 to 3 once.
All inputs are finite; a program needn't handle non-finite values.
Results may differ from a plain program's by a relative error of at most 0.00775.
The roundings to bfloat16 on the way count: a program that leaves them out, or rounds other values in their place, can miss the bound.
Values may be sent and summed in bfloat16 or wider, within the bound.
A program may use at most 128 MiB of HBM per device.

v0:
```python
import math
import jax
import jax.numpy as jnp
from jax import lax
from jax.sharding import PartitionSpec as P

HEAD_DIM = 128
rope_base = 500000.0
floor_value = -1e30


def slot_positions(slot_order, row_ids, span_len):
    slot_ids = jnp.arange(slot_order.shape[0], dtype=jnp.int32)
    picked = jnp.sum(
        jnp.where((row_ids // span_len)[:, None] == slot_ids[None, :], slot_order[None, :], 0),
        axis=1,
    )
    return picked * span_len + row_ids % span_len


def rotate(value_heads, position):
    full_dim = value_heads.shape[-1]
    half_dim = full_dim // 2
    frequency = jnp.float32(rope_base) ** (
        jnp.arange(half_dim, dtype=jnp.float32) * jnp.float32(-2.0 / full_dim)
    )
    angles = position[:, None] * frequency[None, :]
    cosine = jnp.cos(angles)[:, None, :]
    sine_table = jnp.sin(angles)[:, None, :]
    front_half = value_heads[..., :half_dim]
    back_half = value_heads[..., half_dim:]
    return jnp.concatenate(
        [
            front_half * cosine - back_half * sine_table,
            back_half * cosine + front_half * sine_table,
        ],
        axis=-1,
    )


def heads_first(queries, kv_heads, sharing):
    row_count = queries.shape[0]
    shaped = queries.reshape(row_count, kv_heads, sharing, queries.shape[-1])
    return jnp.transpose(shaped, (1, 0, 2, 3)).reshape(
        kv_heads, row_count * sharing, queries.shape[-1]
    )


def empty_state(kv_heads, row_count, head_dim):
    return (
        jnp.full((kv_heads, row_count), floor_value, jnp.float32),
        jnp.zeros((kv_heads, row_count), jnp.float32),
        jnp.zeros((kv_heads, row_count, head_dim), jnp.float32),
    )


def block_update(carried, queries, key_heads, value_heads, allowed):
    running_max, normalizer, weighted = carried
    scaling = 1.0 / math.sqrt(queries.shape[-1])
    scores = (
        jnp.einsum("gqd,kgd->gqk", queries, key_heads, preferred_element_type=jnp.float32) * scaling
    )
    if allowed is not None:
        scores = jnp.where(allowed[None, :, :], scores, -jnp.inf)
    new_max = jnp.maximum(running_max, jnp.max(scores, axis=-1))
    weights = jnp.exp(scores - new_max[..., None])
    shrink = jnp.exp(running_max - new_max)
    normalizer = normalizer * shrink + jnp.sum(weights, axis=-1)
    product = jnp.einsum(
        "gqk,kgd->gqd",
        weights.astype(jnp.bfloat16),
        value_heads,
        preferred_element_type=jnp.float32,
    )
    return (new_max, normalizer, weighted * shrink[..., None] + product)


def key_step(row_count, shard_rows):
    chosen = shard_rows
    factor = 2
    while shard_rows * factor <= 1024 and shard_rows * factor <= row_count:
        if row_count % (shard_rows * factor) == 0:
            chosen = shard_rows * factor
        factor = factor + 1
    return chosen


def run_blocks(
    carried, pieces, first_row, queries, query_pos, slot_order, span_len, shard_rows, masked
):
    row_count = pieces.shape[0]
    block_len = key_step(row_count, shard_rows)
    kv_cols = pieces.shape[1] // 2
    kv_heads = queries.shape[0]
    head_dim = queries.shape[2]
    first_row = jnp.asarray(first_row)

    def one_block(turn_index, inner_state):
        offset = turn_index * block_len
        key_block = lax.dynamic_slice_in_dim(pieces, offset, block_len, 0)
        key_heads = key_block[:, :kv_cols].reshape(block_len, kv_heads, head_dim)
        value_heads = key_block[:, kv_cols:].reshape(block_len, kv_heads, head_dim)
        if not masked:
            return block_update(inner_state, queries, key_heads, value_heads, None)
        key_pos = slot_positions(
            slot_order, offset + jnp.arange(block_len, dtype=jnp.int32), span_len
        )
        allowed = key_pos[None, :] <= query_pos[:, None]
        return block_update(inner_state, queries, key_heads, value_heads, allowed)

    return lax.fori_loop(0, row_count // block_len, one_block, carried)


def finish(carried, row_count, sharing):
    running_max, normalizer, weighted = carried
    kv_heads = weighted.shape[0]
    head_dim = weighted.shape[2]
    result = (weighted / normalizer[..., None]).reshape(kv_heads, row_count, sharing, head_dim)
    return (
        jnp.transpose(result, (1, 0, 2, 3))
        .reshape(row_count, kv_heads * sharing * head_dim)
        .astype(jnp.bfloat16)
    )


def body(hidden_states, query_states, w_query, w_key, w_value, slot_order):
    block_rows, query_rows = (
        lax.all_gather(hidden_states, "tp", axis=0, tiled=True),
        lax.all_gather(query_states, "tp", axis=0, tiled=True),
    )
    qg_count = lax.axis_size("qg")
    member = lax.axis_index("qg")
    blk_index = lax.axis_index("blk")
    head_dim = HEAD_DIM
    heads_local = w_query.shape[1] // head_dim
    kv_heads = w_key.shape[1] // head_dim
    sharing = heads_local // kv_heads
    kv_cols = w_key.shape[1]
    group_rows = block_rows.shape[0]
    span_len = group_rows // 2
    own_rows = group_rows // qg_count
    own_queries = query_rows.shape[0] // qg_count
    columns = block_rows.shape[1]
    seq_len = group_rows * lax.axis_size("blk")
    stacked = jnp.concatenate(
        [
            block_rows.reshape(qg_count, own_rows, columns),
            query_rows.reshape(qg_count, own_queries, columns),
        ],
        axis=1,
    ).reshape(qg_count * (own_rows + own_queries), columns)
    query_sum = lax.psum_scatter(
        jnp.dot(stacked, w_query, preferred_element_type=jnp.float32),
        "qg",
        scatter_dimension=0,
        tiled=True,
    )
    partial_value = jnp.dot(
        block_rows, jnp.concatenate([w_key, w_value], axis=1), preferred_element_type=jnp.float32
    )
    kv_sum = lax.psum(partial_value, "qg")
    kv_start = blk_index * group_rows
    kv_rows = kv_sum.shape[0]
    key_pos = slot_positions(slot_order, kv_start + jnp.arange(kv_rows, dtype=jnp.int32), span_len)
    key_heads = rotate(
        kv_sum[:, :kv_cols].reshape(kv_rows, kv_heads, head_dim), key_pos.astype(jnp.float32)
    )
    kv_cache = jnp.concatenate(
        [
            key_heads.reshape(kv_rows, kv_cols).astype(jnp.bfloat16),
            kv_sum[:, kv_cols:].astype(jnp.bfloat16),
        ],
        axis=1,
    )
    query_start = blk_index * group_rows + member * own_rows
    query_pos = slot_positions(
        slot_order, query_start + jnp.arange(own_rows, dtype=jnp.int32), span_len
    )
    queries = rotate(
        query_sum[:own_rows].reshape(own_rows, heads_local, head_dim), query_pos.astype(jnp.float32)
    ).astype(jnp.bfloat16)
    queries = heads_first(queries, kv_heads, sharing)
    repeated = jnp.repeat(query_pos, sharing)
    fresh_pos = jnp.full((own_queries,), seq_len, jnp.float32)
    decode_query = rotate(
        query_sum[own_rows:].reshape(own_queries, heads_local, head_dim), fresh_pos
    ).astype(jnp.bfloat16)
    asked = heads_first(decode_query, kv_heads, sharing)
    starting = (
        empty_state(kv_heads, own_rows * sharing, head_dim),
        empty_state(kv_heads, own_queries * sharing, head_dim),
    )
    pieces = lax.all_gather(kv_cache, "blk", axis=0, tiled=True)
    first_row = jnp.int32(0)
    prefill_state = run_blocks(
        starting[0], pieces, first_row, queries, repeated, slot_order, span_len, kv_rows, True
    )
    decode_state = run_blocks(
        starting[1], pieces, first_row, asked, None, slot_order, span_len, kv_rows, False
    )
    carried, decode_state = (prefill_state, decode_state)
    decoded = finish(decode_state, own_queries, sharing)
    attention = finish(carried, own_rows, sharing)
    return (attention, decoded)


def solution(mesh):
    return jax.shard_map(
        body,
        mesh=mesh,
        in_specs=(
            P(("blk", "tp"), "qg"),
            P("tp", "qg"),
            P("qg", "tp"),
            P("qg", "tp"),
            P("qg", "tp"),
            P(),
        ),
        out_specs=(P(("blk", "qg"), "tp"), P("qg", "tp")),
        check_vma=False,
    )
```

profile of v0, /device:TPU:0, one launch (start us, length us, event | category | flops | bytes accessed | tf_op | source)
XLA Modules:
  0.0 200.1 jit_solution(10457108261832202985)
XLA Ops:
  7.2 0.7 all-gather.3.cloned.1.call-update
  8.0 41.4 %all-gather.3.cloned.1.call-done = bf16[768,1024]{1,0:T(8,128)(2,1)} async-done(((bf16[192,1024]{1,0:T(8,128)(2,1)}), bf16[768,1024]{1,0:T(8,128)(2,1)}) %all-gather.3.cloned.1.call-update) | async-done | bytes 1572880 | tf_op jit(solution)/shard_map/all_gather | solution.py:128
  49.3 3.9 %convolution_bitcast_fusion = f32[768,512]{0,1:T(8,128)} fusion(bf16[768,1024]{1,0:T(8,128)(2,1)} %all-gather.3.cloned.1.call-done, bf16[1024,256]{1,0:T(8,128)(2,1)} %param.14, bf16[1024,256]{1,0:T(8,128)(2,1)} %param.13), kind=kOutput, calls=%fused_computation.47 | convolution fusion | flops 807403520 | bytes 4194304 | tf_op jit(solution)/shard_map/dot_general | solution.py:158
  53.4 15.9 %all_gather.11 = bf16[256,1024]{1,0:T(8,128)(2,1)S(1)} all-gather(bf16[64,1024]{1,0:T(8,128)(2,1)S(1)} %copy-done.3), channel_id=1, replica_groups=mesh['blk'=2,'tp'=4,'qg'=4] {'tp'}, dimensions={0}, use_global_device_ids=true | all-gather | bytes 655360 | tf_op jit(solution)/shard_map/all_gather | solution.py:129
  69.3 1.7 pad_maximum_fusion
  71.0 4.3 %fusion.46 = f32[1024,1024]{1,0:T(8,128)} fusion(bf16[1024,1024]{1,0:T(8,128)(2,1)S(1)} %bitcast.106, bf16[1024,1024]{1,0:T(8,128)(2,1)S(1)} %copy-done), kind=kOutput, calls=%fused_computation.100 | convolution fusion | flops 2147483648 | bytes 8388608 | tf_op jit(solution)/shard_map/dot_general | solution.py:153
  76.1 0.8 multiply_cosine_fusion
  76.9 18.3 %all-reduce.2.cloned.1.call-done = f32[768,512]{0,1:T(8,128)} async-done(((f32[768,512]{0,1:T(8,128)}), f32[768,512]{0,1:T(8,128)}) %all-reduce.2.cloned.1.call-update) | async-done | bytes 1572880 | tf_op jit(solution)/shard_map/psum | solution.py:161
  95.2 1.2 slice.104
  96.7 0.9 pad_maximum_fusion.1
  98.2 44.2 %reduce-scatter.2.cloned.1.call-done = f32[256,1024]{1,0:T(8,128)} async-done(((f32[1024,1024]{1,0:T(8,128)}), f32[256,1024]{1,0:T(8,128)}) %reduce-scatter.2.cloned.1.call-update) | async-done | bytes 1048592 | tf_op jit(solution)/shard_map/reduce_scatter | solution.py:152
  142.4 1.2 slice_bitcast_fusion
  144.2 0.5 pad_maximum_fusion.3
  144.9 1.0 slice_bitcast_fusion.1
  146.3 24.7 %all-gather.5.cloned.1.call-done = bf16[1536,512]{0,1:T(8,128)(2,1)} async-done(((bf16[768,512]{0,1:T(8,128)(2,1)}), bf16[1536,512]{0,1:T(8,128)(2,1)}) %all-gather.5.cloned.1.call-update) | async-done | bytes 1572880 | tf_op jit(solution)/shard_map/all_gather | solution.py:193
  171.0 4.8 %while.39 = (s32[]{:T(128)}, f32[2,256]{1,0:T(2,128)S(1)}, f32[2,256]{1,0:T(2,128)S(1)}, f32[2,256,128]{2,1,0:T(8,128)S(1)}, bf16[1536,512]{0,1:T(8,128)(2,1)}, ...) while((s32[]{:T(128)}, f32[2,256]{1,0:T(2,128)S(1)}, ...), condition=%wide.region_12.13_spmd.clone, body=%wide.region_9.12_spmd.clone.sunk | while | flops 203885056 | bytes 7766211 | solution.py:111
  171.0 1.2 fusion.90
  173.4 1.2 fusion.90
  176.0 0.7 convert_element_type.74
  176.8 14.2 %while.38 = (s32[]{:T(128)}, f32[2,768]{1,0:T(2,128)S(1)}, f32[2,768]{1,0:T(2,128)S(1)}, f32[2,768,128]{2,1,0:T(8,128)}, s32[4]{0:T(128)S(1)}, /*index=5*/bf16[1...) while((s32[]{:T(128)}, f32[2,768]{1,0:T(2,128)S(1)}, ...), condition=%wide.region_8.9_spmd.clone, body=%wide.region_4.8_spmd.clone.sunk | while | flops 618165504 | bytes 27261984 | solution.py:111
  177.5 1.2 fusion.80
  178.7 1.2 fusion.81
  179.9 1.1 fusion.83
  181.0 1.9 fusion.85
  182.9 0.9 copy-done.2
  184.6 1.2 fusion.80
  185.8 1.2 fusion.81
  187.0 1.1 fusion.83
  188.1 1.9 fusion.85
  190.0 0.9 copy-done.2
  191.0 1.4 divide_convert_fusion
  192.5 1.0 convert_element_type.70
  (78 shorter events, 7.0 us)
Async XLA Ops:
  7.2 63.8 %copy-start = (bf16[1024,1024]{1,0:T(8,128)(2,1)S(1)}, bf16[1024,1024]{1,0:T(8,128)(2,1)}, u32[]{:S(2)}) copy-start(bf16[1024,1024]{1,0:T(8,128)(2,1)} %param.12) | copy-start | bytes 6291460
  7.2 42.2 %all-gather.3.cloned.1.call-start = ((), (), s32[]{:S(2)}) async-start(), calls=%async_computation.1 | async-start | bytes 1966080 | tf_op jit(solution)/shard_map/all_gather | solution.py:128
  7.9 45.4 %copy-start.3 = (bf16[64,1024]{1,0:T(8,128)(2,1)S(1)}, bf16[64,1024]{1,0:T(8,128)(2,1)}, u32[]{:S(2)}) copy-start(bf16[64,1024]{1,0:T(8,128)(2,1)} %param.11) | copy-start | bytes 393220
  7.9 87.3 %all-reduce.2.cloned.1.call-start = ((), (), s32[]{:S(2)}) async-start(), calls=%async_computation.2 | async-start | bytes 3145728 | tf_op jit(solution)/shard_map/psum | solution.py:161
  53.3 89.1 %reduce-scatter.2.cloned.1.call-start = ((), (), s32[]{:S(2)}) async-start(), calls=%async_computation.4 | async-start | bytes 5242880 | tf_op jit(solution)/shard_map/reduce_scatter | solution.py:152
  75.2 0.7 copy-start.4
  75.3 95.7 %all-gather.5.cloned.1.call-start = ((), (), s32[]{:S(2)}) async-start(), calls=%async_computation.3 | async-start | bytes 2359296 | tf_op jit(solution)/shard_map/all_gather | solution.py:193
  95.2 1.4 slice-start
  179.9 1.1 copy-start.1
  182.9 0.9 copy-start.2
  187.0 1.1 copy-start.1
  190.0 0.9 copy-start.2
Sparse Core Ops, SparseCore 0:
  9.6 39.7 all-gather.2
  53.4 41.7 all-reduce.1
  97.7 44.6 reduce-scatter.1
  143.8 27.1 all-gather.4
where the time goes:
time: 201 us; the launch traced here: 200 us
  waiting for transfers between devices  129 us (64%)
  matrix products  16.3 us (8%)
  blocking collectives  15.9 us (8%)
  between operations  14 us (7%)
  local copies, waits for them, and re-layouts  13.1 us (7%)
  other arithmetic  10.8 us (5%)
    reduce_scatter x1, waiting for transfers between devices, body(): lax.psum_scatter(jnp.dot(stacked, w_query, preferred_element_type=jnp.flo...  44.2 us
    all_gather x1, waiting for transfers between devices, body(): lax.all_gather(hidden_states, 'tp', axis=0, tiled=True)  41.4 us
    all_gather x1, waiting for transfers between devices, body(): pieces = lax.all_gather(kv_cache, 'blk', axis=0, tiled=True)  24.7 us
    psum x1, waiting for transfers between devices, body(): kv_sum = lax.psum(partial_value, 'qg')  18.3 us
    all_gather x1, blocking collectives, body(): lax.all_gather(query_states, 'tp', axis=0, tiled=True)  15.9 us
    dot_general x4, matrix products, block_update(): jnp.einsum('gqk,kgd->gqd', weights.astype(jnp.bfloat16), value_heads, pre...  4.86 us
    slice x4, local copies, waits for them, and re-layouts, one_block(): value_heads = key_block[:, kv_cols:].reshape(block_len, kv_heads, head_dim)  4.69 us
    dot_general x1, matrix products, body(): jnp.dot(stacked, w_query, preferred_element_type=jnp.float32)  4.29 us
  transfers between devices with their start and end apart: 4, of which 4 were waited for; matrix products, arithmetic and copies ran while one was open for 7% of the time, Pallas kernels for 0%

commit v1 on v0

--- a/solution.py
+++ b/solution.py
@@ -158,7 +158,8 @@
     partial_value = jnp.dot(
         block_rows, jnp.concatenate([w_key, w_value], axis=1), preferred_element_type=jnp.float32
     )
-    kv_sum = lax.psum(partial_value, "qg")
+    raw_out = lax.all_gather(partial_value, "qg")
+    kv_sum = jnp.sum(raw_out, axis=0)
     kv_start = blk_index * group_rows
     kv_rows = kv_sum.shape[0]
     key_pos = slot_positions(slot_order, kv_start + jnp.arange(kv_rows, dtype=jnp.int32), span_len)

time: 201 us -> 221 us (1.100)
  other arithmetic: 10.8 us -> 27.2 us
  waiting for transfers between devices: 129 us -> 115 us
  local copies, waits for them, and re-layouts: 13.1 us -> 22.4 us
  matrix products: 16.3 us -> 25.4 us
    all_gather x0 -> x1, waiting for transfers between devices: none -> 21.8 us  [body(): raw_out = lax.all_gather(partial_value, 'qg')]
    psum x1 -> x0, waiting for transfers between devices: 18.3 us -> none  [body(): kv_sum = lax.psum(partial_value, 'qg')]
    reduce_scatter x1, waiting for transfers between devices: 44.2 us -> 27.5 us  [body(): lax.psum_scatter(jnp.dot(stacked, w_query, preferred_element_type=jnp.flo...]
    reduce_sum x0 -> x1, other arithmetic: none -> 8.39 us  [body(): kv_sum = jnp.sum(raw_out, axis=0)]
    all_gather x0 -> x1, local copies, waits for them, and re-layouts: none -> 8.3 us  [body(): raw_out = lax.all_gather(partial_value, 'qg')]
    reduce_sum x4, other arithmetic: 2.63 us -> 10.7 us  [block_update(): normalizer = normalizer * shrink + jnp.sum(weights, axis=-1)]
    dot_general x4, matrix products: 3.22 us -> 9.63 us  [block_update(): jnp.einsum('gqd,kgd->gqk', queries, key_heads, preferred_element_type=jnp...]
    dot_general x4, matrix products: 4.86 us -> 7.53 us  [block_update(): jnp.einsum('gqk,kgd->gqd', weights.astype(jnp.bfloat16), value_heads, pre...]
  transfers between devices with their start and end apart: 4 -> 4, of which waited for: 4 -> 4; matrix products, arithmetic and copies ran while one was open for 7% -> 14% of each run, Pallas kernels for 0% -> 0%
where the time goes in v1:
time: 221 us
  waiting for transfers between devices  115 us (52%)
  other arithmetic  27.2 us (12%)
  matrix products  25.4 us (11%)
  local copies, waits for them, and re-layouts  22.4 us (10%)
  blocking collectives  15.9 us (7%)
  between operations  14 us (6%)
    all_gather x1, waiting for transfers between devices, body(): lax.all_gather(hidden_states, 'tp', axis=0, tiled=True)  41.4 us
    reduce_scatter x1, waiting for transfers between devices, body(): lax.psum_scatter(jnp.dot(stacked, w_query, preferred_element_type=jnp.flo...  27.5 us
    all_gather x1, waiting for transfers between devices, body(): pieces = lax.all_gather(kv_cache, 'blk', axis=0, tiled=True)  24.1 us
    all_gather x1, waiting for transfers between devices, body(): raw_out = lax.all_gather(partial_value, 'qg')  21.8 us
    all_gather x1, blocking collectives, body(): lax.all_gather(query_states, 'tp', axis=0, tiled=True)  15.9 us
    reduce_sum x4, other arithmetic, block_update(): normalizer = normalizer * shrink + jnp.sum(weights, axis=-1)  10.7 us
    dot_general x4, matrix products, block_update(): jnp.einsum('gqd,kgd->gqk', queries, key_heads, preferred_element_type=jnp...  9.63 us
    reduce_sum x1, other arithmetic, body(): kv_sum = jnp.sum(raw_out, axis=0)  8.39 us
  transfers between devices with their start and end apart: 4, of which 4 were waited for; matrix products, arithmetic and copies ran while one was open for 14% of the time, Pallas kernels for 0%

profile of v1, /device:TPU:0, one launch (start us, length us, event | category | flops | bytes accessed | tf_op | source)
XLA Modules:
  0.0 220.8 jit_solution(8134922366220937164)
XLA Ops:
  8.0 41.4 %all-gather.5.cloned.1.call-done = bf16[768,1024]{1,0:T(8,128)(2,1)} async-done(((bf16[192,1024]{1,0:T(8,128)(2,1)}), bf16[768,1024]{1,0:T(8,128)(2,1)}) %all-gather.5.cloned.1.call-update) | async-done | bytes 1572880 | tf_op jit(solution)/shard_map/all_gather | solution.py:128
  49.3 3.9 %convolution_bitcast_fusion = f32[768,512]{0,1:T(8,128)} fusion(bf16[768,1024]{1,0:T(8,128)(2,1)} %all-gather.5.cloned.1.call-done, bf16[1024,256]{1,0:T(8,128)(2,1)} %param.14, bf16[1024,256]{1,0:T(8,128)(2,1)} %param.13), kind=kOutput, calls=%fused_computation.47 | convolution fusion | flops 807403520 | bytes 4194304 | tf_op jit(solution)/shard_map/dot_general | solution.py:158
  53.3 15.9 %all_gather.19 = bf16[256,1024]{1,0:T(8,128)(2,1)S(1)} all-gather(bf16[64,1024]{1,0:T(8,128)(2,1)S(1)} %copy-done.6), channel_id=1, replica_groups=mesh['blk'=2,'tp'=4,'qg'=4] {'tp'}, dimensions={0}, use_global_device_ids=true | all-gather | bytes 655360 | tf_op jit(solution)/shard_map/all_gather | solution.py:129
  69.3 1.7 pad_maximum_fusion
  70.9 4.3 %fusion.46 = f32[1024,1024]{1,0:T(8,128)} fusion(bf16[1024,1024]{1,0:T(8,128)(2,1)S(1)} %bitcast.108, bf16[1024,1024]{1,0:T(8,128)(2,1)S(1)} %copy-done), kind=kOutput, calls=%fused_computation.100 | convolution fusion | flops 2147483648 | bytes 8388608 | tf_op jit(solution)/shard_map/dot_general | solution.py:153
  76.9 21.8 %all-gather.9.cloned.1.call-done = f32[3072,512]{0,1:T(8,128)} async-done(((f32[768,512]{0,1:T(8,128)}), f32[3072,512]{0,1:T(8,128)}) %all-gather.9.cloned.1.call-update) | async-done | bytes 6291472 | tf_op jit(solution)/shard_map/all_gather | solution.py:161
  98.7 8.3 %reshape.311 = f32[4,768,512]{1,0,2:T(4,128)} reshape(f32[3072,512]{0,1:T(8,128)} %all-gather.9.cloned.1.call-done) | data formatting | bytes 12582912 | tf_op jit(solution)/shard_map/all_gather | solution.py:161
  107.0 8.4 %reduce_sum.73 = f32[768,512]{0,1:T(8,128)} reduce(f32[4,768,512]{1,0,2:T(4,128)} %reshape.311, f32[]{:T(128)} %constant.189.clone.1), dimensions={0}, to_apply=%region_0.0 | reduce | flops 1179648 | bytes 7864324 | tf_op jit(solution)/shard_map/reduce_sum | solution.py:162
  115.4 1.2 slice.104
  116.9 0.9 pad_maximum_fusion.1
  118.3 27.5 %reduce-scatter.2.cloned.1.call-done = f32[256,1024]{1,0:T(8,128)} async-done(((f32[1024,1024]{1,0:T(8,128)}), f32[256,1024]{1,0:T(8,128)}) %reduce-scatter.2.cloned.1.call-update) | async-done | bytes 1048592 | tf_op jit(solution)/shard_map/reduce_scatter | solution.py:152
  145.8 1.2 slice_bitcast_fusion
  148.3 1.0 slice_bitcast_fusion.1
  150.3 24.1 %all-gather.7.cloned.1.call-done = bf16[1536,512]{0,1:T(8,128)(2,1)} async-done(((bf16[768,512]{0,1:T(8,128)(2,1)}), bf16[1536,512]{0,1:T(8,128)(2,1)}) %all-gather.7.cloned.1.call-update) | async-done | bytes 1572880 | tf_op jit(solution)/shard_map/all_gather | solution.py:194
  174.4 26.0 %while.38 = (s32[]{:T(128)}, f32[2,768]{1,0:T(2,128)S(1)}, f32[2,768]{1,0:T(2,128)S(1)}, f32[2,768,128]{2,1,0:T(8,128)}, s32[4]{0:T(128)S(1)}, /*index=5*/bf16[1...) while((s32[]{:T(128)}, f32[2,768]{1,0:T(2,128)S(1)}, ...), condition=%wide.region_8.9_spmd.clone, body=%wide.region_4.8_spmd.clone.sunk | while | flops 618165504 | bytes 41417752 | solution.py:111
  174.4 1.9 fusion.80
  177.1 3.2 %fusion.81 = (f32[2,768]{1,0:T(2,128)S(1)}, f32[2,768,768]{2,1,0:T(8,128)}) fusion(pred[768,768]{0,1:T(8,128)(4,1)S(1)} %broadcast_compare_fusion.2, bf16[768,2,128]{0,2,1:T(8,128)(2,1)S(1)} %bitcast.99, bf16[2,768,128]{2,1,0:T(8,128)(2,1)S(1)} %get-tuple-element.565), kind=kOutput, calls=%fused_computation.5.clone.1 | convolution fusion | flops 305527296 | bytes 6100992 | tf_op jit(solution)/shard_map/while/body/eval_jaxpr/gqd,kgd->gqk/dot_general | solution.py:61
  180.3 3.6 %fusion.83 = f32[2,768]{1,0:T(2,128)S(1)} fusion(f32[2,768,768]{2,1,0:T(8,128)} %get-tuple-element.517, f32[2,768]{1,0:T(2,128)S(1)} %fusion.82, pred[768,768]{0,1:T(8,128)(4,1)S(1)} %broadcast_compare_fusion.2), kind=kLoop, calls=%fused_computation.4.clone.1 | loop fusion | flops 4717056 | bytes 5320704 | tf_op jit(solution)/shard_map/while/body/eval_jaxpr/reduce_sum | solution.py:68
  184.1 2.7 %fusion.85 = f32[2,768,128]{2,1,0:T(8,128)} fusion(bf16[768,2,128]{0,2,1:T(8,128)(2,1)S(1)} %bitcast.103, f32[2,768,768]{2,1,0:T(8,128)S(1)} %copy-done.1, f32[2,768]{1,0:T(2,128)S(1)} %fusion.82, pred[768,768]{0,1:T(8,128)(4,1)S(1)} %broadcast_compare_fusion.2, f32[2,768,128]{2,1,0:T(8,128)} %get-tuple-element.549, ...), kind=kOutput, calls=%fused_computation.8.clone.1 | convolution fusion | flops 307298304 | bytes 7286785 | tf_op jit(solution)/shard_map/while/body/eval_jaxpr/gqk,kgd->gqd/dot_general | solution.py:69
  186.8 1.9 fusion.80
  189.5 3.2 %fusion.81 = (f32[2,768]{1,0:T(2,128)S(1)}, f32[2,768,768]{2,1,0:T(8,128)}) fusion(pred[768,768]{0,1:T(8,128)(4,1)S(1)} %broadcast_compare_fusion.2, bf16[768,2,128]{0,2,1:T(8,128)(2,1)S(1)} %bitcast.99, bf16[2,768,128]{2,1,0:T(8,128)(2,1)S(1)} %get-tuple-element.565), kind=kOutput, calls=%fused_computation.5.clone.1 | convolution fusion | flops 305527296 | bytes 6100992 | tf_op jit(solution)/shard_map/while/body/eval_jaxpr/gqd,kgd->gqk/dot_general | solution.py:61
  192.7 3.6 %fusion.83 = f32[2,768]{1,0:T(2,128)S(1)} fusion(f32[2,768,768]{2,1,0:T(8,128)} %get-tuple-element.517, f32[2,768]{1,0:T(2,128)S(1)} %fusion.82, pred[768,768]{0,1:T(8,128)(4,1)S(1)} %broadcast_compare_fusion.2), kind=kLoop, calls=%fused_computation.4.clone.1 | loop fusion | flops 4717056 | bytes 5320704 | tf_op jit(solution)/shard_map/while/body/eval_jaxpr/reduce_sum | solution.py:68
  196.6 3.8 %fusion.85 = f32[2,768,128]{2,1,0:T(8,128)} fusion(bf16[768,2,128]{0,2,1:T(8,128)(2,1)S(1)} %bitcast.103, f32[2,768,768]{2,1,0:T(8,128)S(1)} %copy-done.1, f32[2,768]{1,0:T(2,128)S(1)} %fusion.82, pred[768,768]{0,1:T(8,128)(4,1)S(1)} %broadcast_compare_fusion.2, f32[2,768,128]{2,1,0:T(8,128)} %get-tuple-element.549, ...), kind=kOutput, calls=%fused_computation.8.clone.1 | convolution fusion | flops 307298304 | bytes 7286785 | tf_op jit(solution)/shard_map/while/body/eval_jaxpr/gqk,kgd->gqd/dot_general | solution.py:69
  200.4 1.5 divide_convert_fusion
  202.0 1.0 convert_element_type.70
  203.0 10.3 %while.39 = (s32[]{:T(128)}, f32[2,256]{1,0:T(2,128)S(1)}, f32[2,256]{1,0:T(2,128)S(1)}, f32[2,256,128]{2,1,0:T(8,128)S(1)}, bf16[1536,512]{0,1:T(8,128)(2,1)}, ...) while((s32[]{:T(128)}, f32[2,256]{1,0:T(2,128)S(1)}, ...), condition=%wide.region_12.13_spmd.clone, body=%wide.region_9.12_spmd.clone.sunk | while | flops 203885056 | bytes 14057687 | solution.py:111
  203.0 1.2 fusion.90
  204.2 1.6 bitcast_reduce_fusion.2
  205.8 1.8 fusion.92
  208.2 1.2 fusion.90
  209.3 1.6 bitcast_reduce_fusion.2
  210.9 1.8 fusion.92
  (88 shorter events, 9.6 us)
Async XLA Ops:
  7.2 63.8 %copy-start = (bf16[1024,1024]{1,0:T(8,128)(2,1)S(1)}, bf16[1024,1024]{1,0:T(8,128)(2,1)}, u32[]{:S(2)}) copy-start(bf16[1024,1024]{1,0:T(8,128)(2,1)} %param.12) | copy-start | bytes 6291460
  7.2 42.2 %all-gather.5.cloned.1.call-start = ((), (), s32[]{:S(2)}) async-start(), calls=%async_computation.1 | async-start | bytes 1966080 | tf_op jit(solution)/shard_map/all_gather | solution.py:128
  7.9 45.4 %copy-start.6 = (bf16[64,1024]{1,0:T(8,128)(2,1)S(1)}, bf16[64,1024]{1,0:T(8,128)(2,1)}, u32[]{:S(2)}) copy-start(bf16[64,1024]{1,0:T(8,128)(2,1)} %param.11) | copy-start | bytes 393220
  7.9 90.7 %all-gather.9.cloned.1.call-start = ((), (), s32[]{:S(2)}) async-start(), calls=%async_computation.4 | async-start | bytes 7864320 | tf_op jit(solution)/shard_map/all_gather | solution.py:161
  53.3 92.5 %reduce-scatter.2.cloned.1.call-start = ((), (), s32[]{:S(2)}) async-start(), calls=%async_computation.3 | async-start | bytes 5242880 | tf_op jit(solution)/shard_map/reduce_scatter | solution.py:152
  75.2 0.7 copy-start.7
  75.3 99.2 %all-gather.7.cloned.1.call-start = ((), (), s32[]{:S(2)}) async-start(), calls=%async_computation.2 | async-start | bytes 2359296 | tf_op jit(solution)/shard_map/all_gather | solution.py:194
  115.4 1.4 slice-start
  180.3 3.8 %copy-start.1 = (f32[2,768,768]{2,1,0:T(8,128)S(1)}, f32[2,768,768]{2,1,0:T(8,128)}, u32[]{:S(2)}) copy-start(f32[2,768,768]{2,1,0:T(8,128)} %get-tuple-element.517) | copy-start | bytes 14155780 | tf_op jit(solution)/shard_map/while
  180.3 3.8 %copy-start.3 = (bf16[768,256]{0,1:T(8,128)(2,1)S(1)}, bf16[768,256]{0,1:T(8,128)(2,1)}, u32[]{:S(2)}) copy-start(bf16[768,256]{0,1:T(8,128)(2,1)} %get-tuple-element.519) | copy-start | bytes 1179652 | tf_op jit(solution)/shard_map/while
  192.7 3.8 %copy-start.1 = (f32[2,768,768]{2,1,0:T(8,128)S(1)}, f32[2,768,768]{2,1,0:T(8,128)}, u32[]{:S(2)}) copy-start(f32[2,768,768]{2,1,0:T(8,128)} %get-tuple-element.517) | copy-start | bytes 14155780 | tf_op jit(solution)/shard_map/while
  192.7 3.8 %copy-start.3 = (bf16[768,256]{0,1:T(8,128)(2,1)S(1)}, bf16[768,256]{0,1:T(8,128)(2,1)}, u32[]{:S(2)}) copy-start(bf16[768,256]{0,1:T(8,128)(2,1)} %get-tuple-element.519) | copy-start | bytes 1179652 | tf_op jit(solution)/shard_map/while
  200.4 2.6 %copy-start.4 = (f32[2,256,128]{2,1,0:T(8,128)S(1)}, f32[2,256,128]{2,1,0:T(8,128)}, u32[]{:S(2)}) copy-start(f32[2,256,128]{2,1,0:T(8,128)} %custom-call.5) | copy-start | bytes 786436
  200.4 2.6 %copy-start.5 = (bf16[64,2,4,128]{3,2,0,1:T(4,128)(2,1)S(1)}, bf16[64,2,4,128]{3,2,0,1:T(4,128)(2,1)}, u32[]{:S(2)}) copy-start(bf16[64,2,4,128]{3,2,0,1:T(4,128)(2,1)} %copy.47) | copy-start | bytes 393220
  205.7 1.9 copy-start.2
  210.9 1.9 copy-start.2
Sparse Core Ops, SparseCore 0:
  9.6 39.7 all-gather.4
  53.4 45.2 all-gather.8
  101.2 44.5 reduce-scatter.1
  147.2 27.1 all-gather.6
